TPU v7x, 256 devices: a whole 4x4x8 slice. The times are simulated.
256 devices in a mesh: trial: 2 (over core), qa: 16 (over y, x), qb: 8 (over z).
Axes of the slice: x: 4, y: 4, z: 8, core: 2. Of those that a mesh axis runs over, the one named last changes fastest.
Arguments:
- wave_parts: float32 [4, 512, 128, 128], P('trial', ('qa', 'qb')), parts along dimension 0, may hold values from -6 to 6
- level_table: float32 [1024, 128, 128], P(('trial', 'qa', 'qb')), parts along dimension 0, may hold values from -2 to 2
- diagonal_angles: float32 [6, 128], P('trial'), parts along dimension 0, may hold values from 0.3 to 1.2
- turn_angles: float32 [6, 4], P('trial'), parts along dimension 0, may hold values from 0.3 to 1.2
Outputs:
- final_parts: float32 [4, 512, 128, 128], P('trial', ('qa', 'qb')), parts along dimension 0
There are 2 independent parts, one for each index of `trial`. A program takes and returns all parts, laid end to end along the dimension named above; each array names one. Nothing has to cross between parts.
All inputs are finite; a program needn't handle non-finite values.
Results may differ from a plain program's by a relative error of at most 0.0003.
Values sent between devices are 32-bit elements.
A program may use at most 64 MiB of HBM per device.

v0:
```python
import jax
import jax.numpy as jnp
from jax import lax
from jax.sharding import PartitionSpec as P

LAYERS = 3


def count_bits(values, count):
    places = jnp.arange(count.bit_length() - 1, dtype=jnp.int32)
    return jnp.sum(values[..., None] >> places & 1, axis=-1)


def rotation_table(count, angle):
    rank = jnp.arange(count, dtype=jnp.int32)
    apart = count_bits(rank[:, None] ^ rank[None, :], count)
    bits = count.bit_length() - 1
    size = jnp.cos(angle) ** (bits - apart).astype(jnp.float32) * jnp.sin(angle) ** apart.astype(
        jnp.float32
    )
    real_sign = jnp.where(apart % 4 == 0, 1.0, jnp.where(apart % 4 == 2, -1.0, 0.0)).astype(
        jnp.float32
    )
    imag_sign = jnp.where(apart % 4 == 1, -1.0, jnp.where(apart % 4 == 3, 1.0, 0.0)).astype(
        jnp.float32
    )
    return (size * real_sign, size * imag_sign)


def mix_dim(values, dim, angle):
    real_part, imag_part = rotation_table(values.shape[dim], angle)

    def times(table):
        moved = jnp.tensordot(values, table, axes=([dim], [0]), precision=lax.Precision.HIGHEST)
        return jnp.moveaxis(moved, -1, dim)

    by_real = times(real_part)
    by_imag = times(imag_part)
    return jnp.stack([by_real[0] - by_imag[1], by_real[1] + by_imag[0]])


def phase_step(values, levels, angle):
    turn = angle * levels
    return jnp.stack(
        [
            values[0] * jnp.cos(turn) + values[1] * jnp.sin(turn),
            values[1] * jnp.cos(turn) - values[0] * jnp.sin(turn),
        ]
    )


def shards(wave_parts, level_table, diagonal_angles, turn_angles):
    values = wave_parts
    for layer in range(LAYERS):
        values = phase_step(values, level_table, diagonal_angles[layer])
        values = mix_dim(values, 3, turn_angles[layer, 0])
        values = mix_dim(values, 2, turn_angles[layer, 1])
        moved = lax.all_to_all(values, "qa", split_axis=2, concat_axis=1, tiled=True)
        moved = mix_dim(moved, 1, turn_angles[layer, 2])
        values = lax.all_to_all(moved, "qa", split_axis=1, concat_axis=2, tiled=True)
        moved = lax.all_to_all(values, "qb", split_axis=3, concat_axis=1, tiled=True)
        spread = moved.reshape(2, lax.axis_size("qb"), -1, moved.shape[2], moved.shape[3])
        moved = mix_dim(spread, 1, turn_angles[layer, 3]).reshape(moved.shape)
        values = lax.all_to_all(moved, "qb", split_axis=1, concat_axis=3, tiled=True)
    return values


def solution(mesh):
    placed = (
        P("trial", ("qa", "qb"), None, None),
        P(("trial", "qa", "qb"), None, None),
        P("trial", None),
        P("trial", None),
    )
    return jax.shard_map(
        shards,
        mesh=mesh,
        in_specs=placed,
        out_specs=P("trial", ("qa", "qb"), None, None),
        check_vma=False,
    )
```

profile of v0, /device:TPU:2, one launch (start us, length us, event | category | flops | bytes accessed | tf_op | source)
XLA Modules:
  0.0 238.1 jit_solution(5712961371041318198)
XLA Ops:
  0.0 1.8 fusion.327
  3.8 2.0 fusion.19
  9.0 1.1 convolution_bitcast_fusion.17
  10.1 1.1 convolution_bitcast_fusion.16
  12.3 7.5 %all-to-all-start = ((f32[2,4,128,128]{3,1,0,2:T(4,128)}), f32[2,4,128,128]{3,1,0,2:T(4,128)S(1)}, u32[]{:S(2)}, u32[]{:S(2)}) async-start(f32[2,4,128,128]{3,1,0,2:T(4,128)} %copy.169), calls=%async_computation | async-start | bytes 1048576 | tf_op jit(solution)/shard_map/all_to_all | solution.py:58
  21.3 8.6 %all-to-all-done = f32[2,4,128,128]{3,1,0,2:T(4,128)S(1)} async-done(((f32[2,4,128,128]{3,1,0,2:T(4,128)}), f32[2,4,128,128]{3,1,0,2:T(4,128)S(1)}, u32[]{:S(2)}, u32[]{:S(2)}) %all-to-all-start) | async-done | bytes 524320 | tf_op jit(solution)/shard_map/all_to_all | solution.py:58
  32.3 13.8 %all_to_all.201 = f32[2,64,8,128]{3,2,0,1:T(8,128)S(1)} all-to-all(f32[2,64,8,128]{3,2,0,1:T(8,128)S(1)} %copy.174), channel_id=1, replica_groups=mesh['trial'=2,'qa'=16,'qb'=8] {'qa'}, dimensions={1} | all-to-all | bytes 1048576 | tf_op jit(solution)/shard_map/all_to_all | solution.py:60
  47.0 8.4 %all-to-all-start.2 = ((f32[2,4,128,128]{2,1,0,3:T(4,128)}), f32[2,4,128,128]{2,1,0,3:T(4,128)S(1)}, u32[]{:S(2)}, u32[]{:S(2)}) async-start(f32[2,4,128,128]{2,1,0,3:T(4,128)} %copy.177), calls=%async_computation.2 | async-start | bytes 1048576 | tf_op jit(solution)/shard_map/all_to_all | solution.py:61
  57.0 14.2 %all-to-all-done.2 = f32[2,4,128,128]{2,1,0,3:T(4,128)S(1)} async-done(((f32[2,4,128,128]{2,1,0,3:T(4,128)}), f32[2,4,128,128]{2,1,0,3:T(4,128)S(1)}, u32[]{:S(2)}, u32[]{:S(2)}) %all-to-all-start.2) | async-done | bytes 524320 | tf_op jit(solution)/shard_map/all_to_all | solution.py:61
  74.1 3.7 %all-to-all-start.3 = ((f32[2,32,128,16]{2,3,0,1:T(8,128)}), f32[2,32,128,16]{2,3,0,1:T(8,128)S(1)}, u32[]{:S(2)}, u32[]{:S(2)}) async-start(f32[2,32,128,16]{2,3,0,1:T(8,128)} %copy.184), calls=%async_computation.3 | async-start | bytes 1048576 | tf_op jit(solution)/shard_map/all_to_all | solution.py:64
  80.4 11.2 %all-to-all-done.3 = f32[2,32,128,16]{2,3,0,1:T(8,128)S(1)} async-done(((f32[2,32,128,16]{2,3,0,1:T(8,128)}), f32[2,32,128,16]{2,3,0,1:T(8,128)S(1)}, u32[]{:S(2)}, u32[]{:S(2)}) %all-to-all-start.3) | async-done | bytes 524320 | tf_op jit(solution)/shard_map/all_to_all | solution.py:64
  98.7 5.1 %all-to-all-start.4 = ((f32[2,4,128,128]{3,1,0,2:T(4,128)}), f32[2,4,128,128]{3,1,0,2:T(4,128)S(1)}, u32[]{:S(2)}, u32[]{:S(2)}) async-start(f32[2,4,128,128]{3,1,0,2:T(4,128)} %copy.194), calls=%async_computation.4 | async-start | bytes 1048576 | tf_op jit(solution)/shard_map/all_to_all | solution.py:58
  105.2 7.4 %all-to-all-done.4 = f32[2,4,128,128]{3,1,0,2:T(4,128)S(1)} async-done(((f32[2,4,128,128]{3,1,0,2:T(4,128)}), f32[2,4,128,128]{3,1,0,2:T(4,128)S(1)}, u32[]{:S(2)}, u32[]{:S(2)}) %all-to-all-start.4) | async-done | bytes 524320 | tf_op jit(solution)/shard_map/all_to_all | solution.py:58
  114.9 13.1 %all_to_all.202 = f32[2,64,8,128]{3,2,0,1:T(8,128)S(1)} all-to-all(f32[2,64,8,128]{3,2,0,1:T(8,128)S(1)} %copy.199), channel_id=1, replica_groups=mesh['trial'=2,'qa'=16,'qb'=8] {'qa'}, dimensions={1} | all-to-all | bytes 1048576 | tf_op jit(solution)/shard_map/all_to_all | solution.py:60
  129.1 3.5 %all-to-all-start.6 = ((f32[2,4,128,128]{2,1,0,3:T(4,128)}), f32[2,4,128,128]{2,1,0,3:T(4,128)S(1)}, u32[]{:S(2)}, u32[]{:S(2)}) async-start(f32[2,4,128,128]{2,1,0,3:T(4,128)} %copy.202), calls=%async_computation.6 | async-start | bytes 1048576 | tf_op jit(solution)/shard_map/all_to_all | solution.py:61
  133.9 11.9 %all-to-all-done.6 = f32[2,4,128,128]{2,1,0,3:T(4,128)S(1)} async-done(((f32[2,4,128,128]{2,1,0,3:T(4,128)}), f32[2,4,128,128]{2,1,0,3:T(4,128)S(1)}, u32[]{:S(2)}, u32[]{:S(2)}) %all-to-all-start.6) | async-done | bytes 524320 | tf_op jit(solution)/shard_map/all_to_all | solution.py:61
  148.7 3.7 %all-to-all-start.7 = ((f32[2,32,128,16]{2,3,0,1:T(8,128)}), f32[2,32,128,16]{2,3,0,1:T(8,128)S(1)}, u32[]{:S(2)}, u32[]{:S(2)}) async-start(f32[2,32,128,16]{2,3,0,1:T(8,128)} %copy.209), calls=%async_computation.7 | async-start | bytes 1048576 | tf_op jit(solution)/shard_map/all_to_all | solution.py:64
  155.3 10.1 %all-to-all-done.7 = f32[2,32,128,16]{2,3,0,1:T(8,128)S(1)} async-done(((f32[2,32,128,16]{2,3,0,1:T(8,128)}), f32[2,32,128,16]{2,3,0,1:T(8,128)S(1)}, u32[]{:S(2)}, u32[]{:S(2)}) %all-to-all-start.7) | async-done | bytes 524320 | tf_op jit(solution)/shard_map/all_to_all | solution.py:64
  171.8 4.8 %all-to-all-start.8 = ((f32[2,4,128,128]{3,1,0,2:T(4,128)}), f32[2,4,128,128]{3,1,0,2:T(4,128)S(1)}, u32[]{:S(2)}, u32[]{:S(2)}) async-start(f32[2,4,128,128]{3,1,0,2:T(4,128)} %copy.219), calls=%async_computation.8 | async-start | bytes 1048576 | tf_op jit(solution)/shard_map/all_to_all | solution.py:58
  178.0 7.4 %all-to-all-done.8 = f32[2,4,128,128]{3,1,0,2:T(4,128)S(1)} async-done(((f32[2,4,128,128]{3,1,0,2:T(4,128)}), f32[2,4,128,128]{3,1,0,2:T(4,128)S(1)}, u32[]{:S(2)}, u32[]{:S(2)}) %all-to-all-start.8) | async-done | bytes 524320 | tf_op jit(solution)/shard_map/all_to_all | solution.py:58
  187.8 13.1 %all_to_all.203 = f32[2,64,8,128]{3,2,0,1:T(8,128)S(1)} all-to-all(f32[2,64,8,128]{3,2,0,1:T(8,128)S(1)} %copy.224), channel_id=1, replica_groups=mesh['trial'=2,'qa'=16,'qb'=8] {'qa'}, dimensions={1} | all-to-all | bytes 1048576 | tf_op jit(solution)/shard_map/all_to_all | solution.py:60
  201.9 3.5 %all-to-all-start.10 = ((f32[2,4,128,128]{2,1,0,3:T(4,128)}), f32[2,4,128,128]{2,1,0,3:T(4,128)S(1)}, u32[]{:S(2)}, u32[]{:S(2)}) async-start(f32[2,4,128,128]{2,1,0,3:T(4,128)} %copy.227), calls=%async_computation.10 | async-start | bytes 1048576 | tf_op jit(solution)/shard_map/all_to_all | solution.py:61
  206.9 12.3 %all-to-all-done.10 = f32[2,4,128,128]{2,1,0,3:T(4,128)S(1)} async-done(((f32[2,4,128,128]{2,1,0,3:T(4,128)}), f32[2,4,128,128]{2,1,0,3:T(4,128)S(1)}, u32[]{:S(2)}, u32[]{:S(2)}) %all-to-all-start.10) | async-done | bytes 524320 | tf_op jit(solution)/shard_map/all_to_all | solution.py:61
  221.3 15.7 %all_to_all.204 = f32[2,32,128,16]{2,3,0,1:T(8,128)S(1)} all-to-all(f32[2,32,128,16]{2,3,0,1:T(8,128)S(1)} %copy.234), channel_id=1, replica_groups=mesh['trial'=2,'qa'=16,'qb'=8] {'qb'}, dimensions={1} | all-to-all | bytes 1048576 | tf_op jit(solution)/shard_map/all_to_all | solution.py:64
  (97 shorter events, 35.5 us)
Async XLA Ops:
  3.1 0.7 copy-start.1
  12.3 17.6 %all-to-all-start = ((f32[2,4,128,128]{3,1,0,2:T(4,128)}), f32[2,4,128,128]{3,1,0,2:T(4,128)S(1)}, u32[]{:S(2)}, u32[]{:S(2)}) async-start(f32[2,4,128,128]{3,1,0,2:T(4,128)} %copy.169), calls=%async_computation | async-start | bytes 1048576 | tf_op jit(solution)/shard_map/all_to_all | solution.py:58
  47.0 24.1 %all-to-all-start.2 = ((f32[2,4,128,128]{2,1,0,3:T(4,128)}), f32[2,4,128,128]{2,1,0,3:T(4,128)S(1)}, u32[]{:S(2)}, u32[]{:S(2)}) async-start(f32[2,4,128,128]{2,1,0,3:T(4,128)} %copy.177), calls=%async_computation.2 | async-start | bytes 1048576 | tf_op jit(solution)/shard_map/all_to_all | solution.py:61
  74.1 17.5 %all-to-all-start.3 = ((f32[2,32,128,16]{2,3,0,1:T(8,128)}), f32[2,32,128,16]{2,3,0,1:T(8,128)S(1)}, u32[]{:S(2)}, u32[]{:S(2)}) async-start(f32[2,32,128,16]{2,3,0,1:T(8,128)} %copy.184), calls=%async_computation.3 | async-start | bytes 1048576 | tf_op jit(solution)/shard_map/all_to_all | solution.py:64
  91.8 1.0 copy-start
  98.7 13.8 %all-to-all-start.4 = ((f32[2,4,128,128]{3,1,0,2:T(4,128)}), f32[2,4,128,128]{3,1,0,2:T(4,128)S(1)}, u32[]{:S(2)}, u32[]{:S(2)}) async-start(f32[2,4,128,128]{3,1,0,2:T(4,128)} %copy.194), calls=%async_computation.4 | async-start | bytes 1048576 | tf_op jit(solution)/shard_map/all_to_all | solution.py:58
  129.1 16.7 %all-to-all-start.6 = ((f32[2,4,128,128]{2,1,0,3:T(4,128)}), f32[2,4,128,128]{2,1,0,3:T(4,128)S(1)}, u32[]{:S(2)}, u32[]{:S(2)}) async-start(f32[2,4,128,128]{2,1,0,3:T(4,128)} %copy.202), calls=%async_computation.6 | async-start | bytes 1048576 | tf_op jit(solution)/shard_map/all_to_all | solution.py:61
  148.7 16.7 %all-to-all-start.7 = ((f32[2,32,128,16]{2,3,0,1:T(8,128)}), f32[2,32,128,16]{2,3,0,1:T(8,128)S(1)}, u32[]{:S(2)}, u32[]{:S(2)}) async-start(f32[2,32,128,16]{2,3,0,1:T(8,128)} %copy.209), calls=%async_computation.7 | async-start | bytes 1048576 | tf_op jit(solution)/shard_map/all_to_all | solution.py:64
  171.8 13.7 %all-to-all-start.8 = ((f32[2,4,128,128]{3,1,0,2:T(4,128)}), f32[2,4,128,128]{3,1,0,2:T(4,128)S(1)}, u32[]{:S(2)}, u32[]{:S(2)}) async-start(f32[2,4,128,128]{3,1,0,2:T(4,128)} %copy.219), calls=%async_computation.8 | async-start | bytes 1048576 | tf_op jit(solution)/shard_map/all_to_all | solution.py:58
  201.9 17.3 %all-to-all-start.10 = ((f32[2,4,128,128]{2,1,0,3:T(4,128)}), f32[2,4,128,128]{2,1,0,3:T(4,128)S(1)}, u32[]{:S(2)}, u32[]{:S(2)}) async-start(f32[2,4,128,128]{2,1,0,3:T(4,128)} %copy.227), calls=%async_computation.10 | async-start | bytes 1048576 | tf_op jit(solution)/shard_map/all_to_all | solution.py:61
where the time goes:
time: 239 us; the launch traced here: 238 us
  waiting for transfers between devices  83.1 us (35%)
  blocking collectives  55.6 us (23%)
  starting transfers between devices  40.2 us (17%)
  matrix products  20.9 us (9%)
  between operations  17.6 us (7%)
  local copies, waits for them, and re-layouts  15.4 us (6%)
  other arithmetic  5.26 us (2%)
    all_to_all x3, blocking collectives, shards(): lax.all_to_all(moved, 'qa', split_axis=1, concat_axis=2, tiled=True)  39.9 us
    all_to_all x3, waiting for transfers between devices, shards(): lax.all_to_all(values, 'qb', split_axis=3, concat_axis=1, tiled=True)  38.4 us
    all_to_all x3, waiting for transfers between devices, shards(): lax.all_to_all(values, 'qa', split_axis=2, concat_axis=1, tiled=True)  23.4 us
    all_to_all x2, waiting for transfers between devices, shards(): lax.all_to_all(moved, 'qb', split_axis=1, concat_axis=3, tiled=True)  21.3 us
    dot_general x24, matrix products, times(): jnp.tensordot(values, table, axes=([dim], [0]), precision=lax.Precision.H...  20.9 us
    all_to_all x3, starting transfers between devices, shards(): lax.all_to_all(values, 'qa', split_axis=2, concat_axis=1, tiled=True)  17.4 us
    all_to_all x1, blocking collectives, shards(): lax.all_to_all(moved, 'qb', split_axis=1, concat_axis=3, tiled=True)  15.7 us
    all_to_all x3, starting transfers between devices, shards(): lax.all_to_all(values, 'qb', split_axis=3, concat_axis=1, tiled=True)  15.4 us
  transfers between devices with their start and end apart: 8, of which 8 were waited for; matrix products, arithmetic and copies ran while one was open for 0% of the time, Pallas kernels for 0%

commit v1 on v0

--- a/solution.py
+++ b/solution.py
@@ -61,7 +61,13 @@
         moved = lax.all_to_all(values, "qb", split_axis=3, concat_axis=1, tiled=True)
         spread = moved.reshape(2, lax.axis_size("qb"), -1, moved.shape[2], moved.shape[3])
         moved = mix_dim(spread, 1, turn_angles[layer, 3]).reshape(moved.shape)
-        values = lax.all_to_all(moved, "qb", split_axis=1, concat_axis=3, tiled=True)
+        bind_series = lambda row_data: jnp.concatenate(
+            jax.lax.all_to_all(
+                jnp.stack(jnp.split(row_data, jax.lax.axis_size("qb"), axis=1), axis=0), "qb", 0, 0
+            ),
+            axis=3,
+        )
+        values = bind_series(moved)
     return values
 
 

time: 239 us -> 248 us (1.038)
  other arithmetic: 5.26 us -> 15.4 us
    unnamed x0 -> x21, other arithmetic: none -> 8.93 us
    another operation x9 -> x6, local copies, waits for them, and re-layouts: 5.69 us -> 3.91 us  [mix_dim(): return jnp.stack([by_real[0] - by_imag[1], by_real[1] + by_imag[0]])]
where the time goes in v1:
time: 248 us; the launch traced here: 247 us
  waiting for transfers between devices  83.5 us (34%)
  blocking collectives  55.7 us (22%)
  starting transfers between devices  40.2 us (16%)
  matrix products  20.9 us (8%)
  between operations  17.6 us (7%)
  other arithmetic  15.4 us (6%)
  local copies, waits for them, and re-layouts  13.6 us (5%)
    all_to_all x3, blocking collectives, shards(): lax.all_to_all(moved, 'qa', split_axis=1, concat_axis=2, tiled=True)  39.9 us
    all_to_all x3, waiting for transfers between devices, shards(): lax.all_to_all(values, 'qb', split_axis=3, concat_axis=1, tiled=True)  38.7 us
    all_to_all x3, waiting for transfers between devices, shards(): lax.all_to_all(values, 'qa', split_axis=2, concat_axis=1, tiled=True)  23.5 us
    all_to_all x2, waiting for transfers between devices, shards(): jax.lax.all_to_all(jnp.stack(jnp.split(row_data, jax.lax.axis_size('qb'),...  21.3 us
    dot_general x24, matrix products, times(): jnp.tensordot(values, table, axes=([dim], [0]), precision=lax.Precision.H...  20.9 us
    all_to_all x3, starting transfers between devices, shards(): lax.all_to_all(values, 'qa', split_axis=2, concat_axis=1, tiled=True)  17.3 us
    all_to_all x1, blocking collectives, shards(): jax.lax.all_to_all(jnp.stack(jnp.split(row_data, jax.lax.axis_size('qb'),...  15.8 us
    all_to_all x3, starting transfers between devices, shards(): lax.all_to_all(values, 'qb', split_axis=3, concat_axis=1, tiled=True)  15.4 us
  transfers between devices with their start and end apart: 8, of which 8 were waited for; matrix products, arithmetic and copies ran while one was open for 0% of the time, Pallas kernels for 0%

profile of v1, /device:TPU:2, one launch (start us, length us, event | category | flops | bytes accessed | tf_op | source)
XLA Modules:
  0.0 246.8 jit_solution(2366360164211526729)
XLA Ops:
  0.0 1.8 fusion.396
  3.8 2.0 fusion.19
  9.0 1.1 convolution_bitcast_fusion.17
  12.3 7.5 %all-to-all-start = ((f32[2,4,128,128]{3,1,0,2:T(4,128)}), f32[2,4,128,128]{3,1,0,2:T(4,128)S(1)}, u32[]{:S(2)}, u32[]{:S(2)}) async-start(f32[2,4,128,128]{3,1,0,2:T(4,128)} %copy.178), calls=%async_computation | async-start | bytes 1048576 | tf_op jit(solution)/shard_map/all_to_all | solution.py:58
  21.3 8.6 %all-to-all-done = f32[2,4,128,128]{3,1,0,2:T(4,128)S(1)} async-done(((f32[2,4,128,128]{3,1,0,2:T(4,128)}), f32[2,4,128,128]{3,1,0,2:T(4,128)S(1)}, u32[]{:S(2)}, u32[]{:S(2)}) %all-to-all-start) | async-done | bytes 524320 | tf_op jit(solution)/shard_map/all_to_all | solution.py:58
  32.3 13.8 %all_to_all.168 = f32[2,64,8,128]{3,2,0,1:T(8,128)S(1)} all-to-all(f32[2,64,8,128]{3,2,0,1:T(8,128)S(1)} %copy.183), channel_id=1, replica_groups=mesh['trial'=2,'qa'=16,'qb'=8] {'qa'}, dimensions={1} | all-to-all | bytes 1048576 | tf_op jit(solution)/shard_map/all_to_all | solution.py:60
  47.0 8.5 %all-to-all-start.2 = ((f32[2,4,128,128]{2,1,0,3:T(4,128)}), f32[2,4,128,128]{2,1,0,3:T(4,128)S(1)}, u32[]{:S(2)}, u32[]{:S(2)}) async-start(f32[2,4,128,128]{2,1,0,3:T(4,128)} %copy.186), calls=%async_computation.2 | async-start | bytes 1048576 | tf_op jit(solution)/shard_map/all_to_all | solution.py:61
  57.0 14.2 %all-to-all-done.2 = f32[2,4,128,128]{2,1,0,3:T(4,128)S(1)} async-done(((f32[2,4,128,128]{2,1,0,3:T(4,128)}), f32[2,4,128,128]{2,1,0,3:T(4,128)S(1)}, u32[]{:S(2)}, u32[]{:S(2)}) %all-to-all-start.2) | async-done | bytes 524320 | tf_op jit(solution)/shard_map/all_to_all | solution.py:61
  78.2 3.7 %all-to-all-start.3 = ((f32[8,2,4,128,16]{3,4,2,1,0:T(8,128)}), f32[8,2,4,128,16]{3,4,2,1,0:T(8,128)S(1)}, u32[]{:S(2)}, u32[]{:S(2)}) async-start(f32[8,2,4,128,16]{3,4,2,1,0:T(8,128)} %fusion.91), calls=%async_computation.3 | async-start | bytes 1048576 | tf_op jit(solution)/shard_map/all_to_all | solution.py:65
  84.6 11.2 %all-to-all-done.3 = f32[8,2,4,128,16]{3,4,2,1,0:T(8,128)S(1)} async-done(((f32[8,2,4,128,16]{3,4,2,1,0:T(8,128)}), f32[8,2,4,128,16]{3,4,2,1,0:T(8,128)S(1)}, u32[]{:S(2)}, u32[]{:S(2)}) %all-to-all-start.3) | async-done | bytes 524320 | tf_op jit(solution)/shard_map/all_to_all | solution.py:65
  102.9 5.0 %all-to-all-start.4 = ((f32[2,4,128,128]{3,1,0,2:T(4,128)}), f32[2,4,128,128]{3,1,0,2:T(4,128)S(1)}, u32[]{:S(2)}, u32[]{:S(2)}) async-start(f32[2,4,128,128]{3,1,0,2:T(4,128)} %copy.201), calls=%async_computation.4 | async-start | bytes 1048576 | tf_op jit(solution)/shard_map/all_to_all | solution.py:58
  109.3 7.4 %all-to-all-done.4 = f32[2,4,128,128]{3,1,0,2:T(4,128)S(1)} async-done(((f32[2,4,128,128]{3,1,0,2:T(4,128)}), f32[2,4,128,128]{3,1,0,2:T(4,128)S(1)}, u32[]{:S(2)}, u32[]{:S(2)}) %all-to-all-start.4) | async-done | bytes 524320 | tf_op jit(solution)/shard_map/all_to_all | solution.py:58
  119.1 13.1 %all_to_all.169 = f32[2,64,8,128]{3,2,0,1:T(8,128)S(1)} all-to-all(f32[2,64,8,128]{3,2,0,1:T(8,128)S(1)} %copy.206), channel_id=1, replica_groups=mesh['trial'=2,'qa'=16,'qb'=8] {'qa'}, dimensions={1} | all-to-all | bytes 1048576 | tf_op jit(solution)/shard_map/all_to_all | solution.py:60
  133.2 3.5 %all-to-all-start.6 = ((f32[2,4,128,128]{2,1,0,3:T(4,128)}), f32[2,4,128,128]{2,1,0,3:T(4,128)S(1)}, u32[]{:S(2)}, u32[]{:S(2)}) async-start(f32[2,4,128,128]{2,1,0,3:T(4,128)} %copy.209), calls=%async_computation.6 | async-start | bytes 1048576 | tf_op jit(solution)/shard_map/all_to_all | solution.py:61
  138.0 11.9 %all-to-all-done.6 = f32[2,4,128,128]{2,1,0,3:T(4,128)S(1)} async-done(((f32[2,4,128,128]{2,1,0,3:T(4,128)}), f32[2,4,128,128]{2,1,0,3:T(4,128)S(1)}, u32[]{:S(2)}, u32[]{:S(2)}) %all-to-all-start.6) | async-done | bytes 524320 | tf_op jit(solution)/shard_map/all_to_all | solution.py:61
  157.0 3.7 %all-to-all-start.7 = ((f32[8,2,4,128,16]{3,4,2,1,0:T(8,128)}), f32[8,2,4,128,16]{3,4,2,1,0:T(8,128)S(1)}, u32[]{:S(2)}, u32[]{:S(2)}) async-start(f32[8,2,4,128,16]{3,4,2,1,0:T(8,128)} %fusion.89), calls=%async_computation.7 | async-start | bytes 1048576 | tf_op jit(solution)/shard_map/all_to_all | solution.py:65
  163.6 10.1 %all-to-all-done.7 = f32[8,2,4,128,16]{3,4,2,1,0:T(8,128)S(1)} async-done(((f32[8,2,4,128,16]{3,4,2,1,0:T(8,128)}), f32[8,2,4,128,16]{3,4,2,1,0:T(8,128)S(1)}, u32[]{:S(2)}, u32[]{:S(2)}) %all-to-all-start.7) | async-done | bytes 524320 | tf_op jit(solution)/shard_map/all_to_all | solution.py:65
  176.8 1.1 convolution_bitcast_fusion.5
  180.1 4.8 %all-to-all-start.8 = ((f32[2,4,128,128]{3,1,0,2:T(4,128)}), f32[2,4,128,128]{3,1,0,2:T(4,128)S(1)}, u32[]{:S(2)}, u32[]{:S(2)}) async-start(f32[2,4,128,128]{3,1,0,2:T(4,128)} %copy.224), calls=%async_computation.8 | async-start | bytes 1048576 | tf_op jit(solution)/shard_map/all_to_all | solution.py:58
  186.3 7.4 %all-to-all-done.8 = f32[2,4,128,128]{3,1,0,2:T(4,128)S(1)} async-done(((f32[2,4,128,128]{3,1,0,2:T(4,128)}), f32[2,4,128,128]{3,1,0,2:T(4,128)S(1)}, u32[]{:S(2)}, u32[]{:S(2)}) %all-to-all-start.8) | async-done | bytes 524320 | tf_op jit(solution)/shard_map/all_to_all | solution.py:58
  196.1 13.1 %all_to_all.170 = f32[2,64,8,128]{3,2,0,1:T(8,128)S(1)} all-to-all(f32[2,64,8,128]{3,2,0,1:T(8,128)S(1)} %copy.229), channel_id=1, replica_groups=mesh['trial'=2,'qa'=16,'qb'=8] {'qa'}, dimensions={1} | all-to-all | bytes 1048576 | tf_op jit(solution)/shard_map/all_to_all | solution.py:60
  210.2 3.5 %all-to-all-start.10 = ((f32[2,4,128,128]{2,1,0,3:T(4,128)}), f32[2,4,128,128]{2,1,0,3:T(4,128)S(1)}, u32[]{:S(2)}, u32[]{:S(2)}) async-start(f32[2,4,128,128]{2,1,0,3:T(4,128)} %copy.232), calls=%async_computation.10 | async-start | bytes 1048576 | tf_op jit(solution)/shard_map/all_to_all | solution.py:61
  215.3 12.7 %all-to-all-done.10 = f32[2,4,128,128]{2,1,0,3:T(4,128)S(1)} async-done(((f32[2,4,128,128]{2,1,0,3:T(4,128)}), f32[2,4,128,128]{2,1,0,3:T(4,128)S(1)}, u32[]{:S(2)}, u32[]{:S(2)}) %all-to-all-start.10) | async-done | bytes 524320 | tf_op jit(solution)/shard_map/all_to_all | solution.py:61
  230.0 15.8 %all_to_all.171 = f32[8,2,4,128,16]{3,4,2,1,0:T(8,128)S(1)} all-to-all(f32[8,2,4,128,16]{3,4,2,1,0:T(8,128)S(1)} %fusion.87), channel_id=1, replica_groups=mesh['trial'=2,'qa'=16,'qb'=8] {'qb'}, dimensions={0} | all-to-all | bytes 1048576 | tf_op jit(solution)/shard_map/all_to_all | solution.py:65
  (113 shorter events, 43.8 us)
Async XLA Ops:
  3.1 0.7 copy-start.1
  12.3 17.6 %all-to-all-start = ((f32[2,4,128,128]{3,1,0,2:T(4,128)}), f32[2,4,128,128]{3,1,0,2:T(4,128)S(1)}, u32[]{:S(2)}, u32[]{:S(2)}) async-start(f32[2,4,128,128]{3,1,0,2:T(4,128)} %copy.178), calls=%async_computation | async-start | bytes 1048576 | tf_op jit(solution)/shard_map/all_to_all | solution.py:58
  47.0 24.1 %all-to-all-start.2 = ((f32[2,4,128,128]{2,1,0,3:T(4,128)}), f32[2,4,128,128]{2,1,0,3:T(4,128)S(1)}, u32[]{:S(2)}, u32[]{:S(2)}) async-start(f32[2,4,128,128]{2,1,0,3:T(4,128)} %copy.186), calls=%async_computation.2 | async-start | bytes 1048576 | tf_op jit(solution)/shard_map/all_to_all | solution.py:61
  78.2 17.5 %all-to-all-start.3 = ((f32[8,2,4,128,16]{3,4,2,1,0:T(8,128)}), f32[8,2,4,128,16]{3,4,2,1,0:T(8,128)S(1)}, u32[]{:S(2)}, u32[]{:S(2)}) async-start(f32[8,2,4,128,16]{3,4,2,1,0:T(8,128)} %fusion.91), calls=%async_computation.3 | async-start | bytes 1048576 | tf_op jit(solution)/shard_map/all_to_all | solution.py:65
  96.0 1.0 copy-start
  102.9 13.9 %all-to-all-start.4 = ((f32[2,4,128,128]{3,1,0,2:T(4,128)}), f32[2,4,128,128]{3,1,0,2:T(4,128)S(1)}, u32[]{:S(2)}, u32[]{:S(2)}) async-start(f32[2,4,128,128]{3,1,0,2:T(4,128)} %copy.201), calls=%async_computation.4 | async-start | bytes 1048576 | tf_op jit(solution)/shard_map/all_to_all | solution.py:58
  133.2 16.7 %all-to-all-start.6 = ((f32[2,4,128,128]{2,1,0,3:T(4,128)}), f32[2,4,128,128]{2,1,0,3:T(4,128)S(1)}, u32[]{:S(2)}, u32[]{:S(2)}) async-start(f32[2,4,128,128]{2,1,0,3:T(4,128)} %copy.209), calls=%async_computation.6 | async-start | bytes 1048576 | tf_op jit(solution)/shard_map/all_to_all | solution.py:61
  157.0 16.7 %all-to-all-start.7 = ((f32[8,2,4,128,16]{3,4,2,1,0:T(8,128)}), f32[8,2,4,128,16]{3,4,2,1,0:T(8,128)S(1)}, u32[]{:S(2)}, u32[]{:S(2)}) async-start(f32[8,2,4,128,16]{3,4,2,1,0:T(8,128)} %fusion.89), calls=%async_computation.7 | async-start | bytes 1048576 | tf_op jit(solution)/shard_map/all_to_all | solution.py:65
  180.1 13.7 %all-to-all-start.8 = ((f32[2,4,128,128]{3,1,0,2:T(4,128)}), f32[2,4,128,128]{3,1,0,2:T(4,128)S(1)}, u32[]{:S(2)}, u32[]{:S(2)}) async-start(f32[2,4,128,128]{3,1,0,2:T(4,128)} %copy.224), calls=%async_computation.8 | async-start | bytes 1048576 | tf_op jit(solution)/shard_map/all_to_all | solution.py:58
  210.2 17.7 %all-to-all-start.10 = ((f32[2,4,128,128]{2,1,0,3:T(4,128)}), f32[2,4,128,128]{2,1,0,3:T(4,128)S(1)}, u32[]{:S(2)}, u32[]{:S(2)}) async-start(f32[2,4,128,128]{2,1,0,3:T(4,128)} %copy.232), calls=%async_computation.10 | async-start | bytes 1048576 | tf_op jit(solution)/shard_map/all_to_all | solution.py:61
